TPU v7x, 32 devices: a whole 2x2x4 slice. The times are simulated.
32 devices in a mesh: rep: 2 (over y), gx: 16 (over z, x, core).
Axes of the slice: x: 2, y: 2, z: 4, core: 2. Of those that a mesh axis runs over, the one named last changes fastest.
Arguments:
- positions: float32 [3, 49152], P(None, ('rep', 'gx')), parts along dimension 1, may hold values from 0 to 96
- velocities: float32 [3, 49152], P(None, ('rep', 'gx')), parts along dimension 1, may hold values from -9 to 9
- atom_params: float32 [4, 49152], P(None, ('rep', 'gx')), parts along dimension 1, may hold values from -1 to 2, as said below
- pair_list: int32 [3, 540672], P(None, ('rep', 'gx')), parts along dimension 1, may hold values from 0 to 479, as said below
- pair_count: int32 [32], P(('rep', 'gx')), parts along dimension 0, may hold values from 2112 to 16896, as said below
- exclusion: int32 [4, 540672], P(None, ('rep', 'gx')), parts along dimension 1, may hold values from 0 to 65535, as said below
- halo_far: int32 [3072], P(('rep', 'gx')), parts along dimension 0, may hold values from 0 to 191, as said below
- box_lengths: float32 [6], P('rep'), parts along dimension 0, may hold values from 12 to 96
- extended_variables: float32 [8], P('rep'), parts along dimension 0, may hold values from -0.3 to 0.3
Outputs:
- forces: float32 [3, 49152], P(None, ('rep', 'gx')), parts along dimension 1
- new_velocities: float32 [3, 49152], P(None, ('rep', 'gx')), parts along dimension 1
- new_positions: float32 [3, 49152], P(None, ('rep', 'gx')), parts along dimension 1
- new_coupling: float32 [8], P('rep'), parts along dimension 0
There are 2 independent parts, one for each index of `rep`. A program takes and returns all parts, laid end to end along the dimension named above; each array names one. Nothing has to cross between parts.
Inputs may be any that keep to these rules, and one draw needn't show every extreme that they name: `pair_list`: row 0 is a local cluster 0 to 191, row 1 a slot 0 to 479 of the slot table, row 2 an image code 0 to 8. Over each domain's used columns row 0 never falls (the list is grouped by its first cluster). Unused columns hold valid entries too. `pair_count`: at most 16896; some domain uses all 16896 columns in every draw. `exclusion`: each word holds 16 bits; bit 1 means the atom pair interacts. `halo_far`: 96 distinct local clusters of each domain. `atom_params`: rows 1 to 3 are positive.
All inputs are finite; a program needn't handle non-finite values.
Results may differ from a plain program's by a relative error of at most 0.0003.
Values sent between devices are 32-bit elements; how exact they have to be, the bound alone decides.
A program may use at most 64 MiB of HBM per device.

v0:
```python
import jax
import jax.numpy as jnp
from jax import lax
from jax.sharding import PartitionSpec as P

LY = 12
time_step = 0.25
reaction_term = 1.0 / 1331.0
thermal_scale_unit = 2.0
reservoir_inertia_mass = 4.0
barostat_gain = 0.1
pressure_target = 1.0


def passed_along(value, axis, steps):
    count = lax.axis_size(axis)
    pairs = [(source, (source + steps) % count) for source in range(count)]
    return lax.ppermute(value, axis, pairs)


def pair_tiles(slot_table, pair_rows, word_rows, usable, box_lengths):
    tile_width = pair_rows.shape[1]
    first_rows = jnp.take(slot_table, pair_rows[0], axis=0).T.reshape(6, 8, tile_width)
    second_rows = jnp.take(slot_table, pair_rows[1], axis=0).T.reshape(6, 8, tile_width)
    image_y = (pair_rows[2] // 3 - 1).astype(jnp.float32) * box_lengths[1]
    image_z = (pair_rows[2] % 3 - 1).astype(jnp.float32) * box_lengths[2]
    delta_x = second_rows[0][None, :, :] - first_rows[0][:, None, :]
    delta_y = second_rows[1][None, :, :] - first_rows[1][:, None, :] + image_y
    delta_z = second_rows[2][None, :, :] - first_rows[2][:, None, :] + image_z
    shifts = (jnp.arange(64, dtype=jnp.int32) % 16)[:, None]
    mask_bits = jnp.right_shift(jnp.repeat(word_rows, 16, axis=0), shifts) & 1
    interact = (mask_bits.reshape(8, 8, tile_width) == 1) & usable[None, None, :]
    radius_sq = delta_x * delta_x + delta_y * delta_y + delta_z * delta_z
    radius_sq = jnp.where(interact, radius_sq, 1.0)
    inverse = lax.rsqrt(radius_sq)
    inverse_sq = inverse * inverse
    inverse_six = inverse_sq * inverse_sq * inverse_sq
    charge_pair = first_rows[3][:, None, :] * second_rows[3][None, :, :]
    dispersion = first_rows[4][:, None, :] * second_rows[4][None, :, :]
    repulsion = first_rows[5][:, None, :] * second_rows[5][None, :, :]
    scalar = (
        charge_pair * (inverse * inverse_sq - reaction_term)
        + (12.0 * repulsion * inverse_six - 6.0 * dispersion) * inverse_six * inverse_sq
    )
    scalar = jnp.where(interact, scalar, 0.0)
    components = (delta_x, delta_y, delta_z)
    onto_second = jnp.stack([jnp.sum(scalar * component, axis=0) for component in components])
    onto_first = -jnp.stack([jnp.sum(scalar * component, axis=1) for component in components])
    virial = -0.5 * jnp.stack([jnp.sum(scalar * component * component) for component in components])
    tile_terms = jnp.concatenate(
        [onto_first.reshape(24, tile_width), onto_second.reshape(24, tile_width)], axis=1
    ).T
    owners = jnp.concatenate([pair_rows[0], pair_rows[1]])
    return (tile_terms, owners, virial)


def on_device(
    positions,
    velocities,
    atom_params,
    pair_list,
    pair_count,
    exclusion,
    halo_far,
    box_lengths,
    extended_variables,
):
    atoms_here = positions.shape[1]
    clusters = atoms_here // 8
    far_clusters = halo_far.shape[0]
    slots = 2 * clusters + far_clusters
    block_rows = pair_list.shape[1] // LY
    domain_index = lax.axis_index("gx")
    axis_count = lax.axis_size("gx")
    inverse_mass = atom_params[3]
    kinetic = 0.5 * jnp.sum(velocities * velocities / inverse_mass[None, :], axis=1)
    overall_motion_work = lax.psum(kinetic, "gx")
    packed = jnp.concatenate([positions, atom_params[:3]], axis=0)
    far_rows = packed.reshape(6, clusters, 8)[:, halo_far, :].reshape(6, far_clusters * 8)
    near_rows = passed_along(packed, "gx", -1)
    far_in = passed_along(far_rows, "gx", -2)
    near_rows = near_rows.at[0].add(jnp.where(domain_index == axis_count - 1, box_lengths[0], 0.0))
    far_in = far_in.at[0].add(jnp.where(domain_index >= axis_count - 2, box_lengths[0], 0.0))
    slot_table = jnp.concatenate([packed, near_rows, far_in], axis=1)
    slot_table = slot_table.reshape(6, slots, 8).transpose(1, 0, 2).reshape(slots, 48)
    pair_total = pair_count[0]
    slot_numbers = jnp.arange(slots, dtype=jnp.int32)[:, None]

    def one_block(block_index, running):
        accumulated, virial = running
        first_row = block_index * block_rows
        pair_block = lax.dynamic_slice_in_dim(pair_list, first_row, block_rows, 1)
        word_block = lax.dynamic_slice_in_dim(exclusion, first_row, block_rows, 1)
        usable = first_row + jnp.arange(block_rows, dtype=jnp.int32) < pair_total
        tile_terms, owners, partial_value = pair_tiles(
            slot_table, pair_block, word_block, usable, box_lengths
        )
        selector = (slot_numbers == owners[None, :]).astype(jnp.float32)
        accumulated = accumulated + jnp.dot(
            selector,
            tile_terms,
            precision=lax.Precision.HIGHEST,
            preferred_element_type=jnp.float32,
        )
        return (accumulated, virial + partial_value)

    block_count = (pair_total + block_rows - 1) // block_rows
    start_state = (jnp.zeros((slots, 24), jnp.float32), jnp.zeros((3,), jnp.float32))
    accumulated, virial = lax.fori_loop(0, block_count, one_block, start_state)
    columns = accumulated.T
    near_back = passed_along(columns[:, clusters : 2 * clusters], "gx", 1)
    far_back = passed_along(columns[:, 2 * clusters :], "gx", 2)
    summed = columns[:, :clusters] + near_back
    summed = summed.at[:, halo_far].add(far_back)
    forces = summed.reshape(3, 8, clusters).transpose(0, 2, 1).reshape(3, atoms_here)
    virial_total = lax.psum(virial, "gx")
    combined_potential = jnp.sum(overall_motion_work)
    particle_number_overall = atoms_here * axis_count
    volume = box_lengths[0] * box_lengths[1] * box_lengths[2]
    thermal_ratio_value = (
        2.0 * combined_potential / (3.0 * particle_number_overall * thermal_scale_unit)
    )
    reservoir_damping = extended_variables[0] + reservoir_inertia_mass * (thermal_ratio_value - 1.0)
    box_rates = extended_variables[1:] + barostat_gain * (
        overall_motion_work - virial_total - pressure_target * volume / 2.0
    ) / (combined_potential / 3.0)
    new_velocities = velocities + time_step * (
        forces * inverse_mass[None, :] - (reservoir_damping + box_rates[:, None]) * velocities
    )
    new_positions = positions * (1.0 + time_step * box_rates[:, None]) + time_step * new_velocities
    new_coupling = jnp.concatenate([reservoir_damping[None], box_rates])
    return (forces, new_velocities, new_positions, new_coupling)


def solution(mesh):
    return jax.shard_map(
        on_device,
        mesh=mesh,
        in_specs=(
            P(None, ("rep", "gx")),
            P(None, ("rep", "gx")),
            P(None, ("rep", "gx")),
            P(None, ("rep", "gx")),
            P(("rep", "gx")),
            P(None, ("rep", "gx")),
            P(("rep", "gx")),
            P("rep"),
            P("rep"),
        ),
        out_specs=(
            P(None, ("rep", "gx")),
            P(None, ("rep", "gx")),
            P(None, ("rep", "gx")),
            P("rep"),
        ),
        check_vma=False,
    )
```

profile of v0, /device:TPU:0, one launch (start us, length us, event | category | flops | bytes accessed | tf_op | source)
XLA Modules:
  0.0 471.5 jit_solution(7879650573326393458)
XLA Ops:
  1.4 5.5 %collective-permute-start = (f32[6,1536]{1,0:T(8,128)S(1)}, f32[6,1536]{1,0:T(8,128)S(1)}, u32[]{:S(2)}, u32[]{:S(2)}) collective-permute-start(f32[6,1536]{1,0:T(8,128)S(1)} %pad_maximum_fusion.1), channel_id=1, source_target_pairs={{0,15},{1,0},{2,1},{3,2},{4,3},{5,4},{6,5},{7,6},{8,7},{9,8},{10,9... | collective-permute-start | bytes 110600 | tf_op jit(solution)/shard_map/ppermute | solution.py:18
  18.8 408.7 %while.18 = (s32[]{:T(128)}, f32[480,24]{0,1:T(8,128)}, f32[3]{0:T(128)}, s32[]{:T(128)}, s32[3,16896]{1,0:T(4,128)}, /*index=5*/s32[4,16896]{1,0:T(4,128)}, s32...) while((s32[]{:T(128)}, f32[480,24]{0,1:T(8,128)}, ...), condition=%wide.region_10.12_spmd.clone, body=%wide.region_0.11_spmd.clone.sunk | while | flops 397501280 | bytes 8990699 | solution.py:109
  26.0 2.7 gather_fusion.1
  29.0 2.7 gather_fusion
  60.0 2.7 gather_fusion.1
  63.0 2.7 gather_fusion
  94.2 2.7 gather_fusion.1
  97.1 2.7 gather_fusion
  128.2 2.7 gather_fusion.1
  131.2 2.7 gather_fusion
  162.3 2.7 gather_fusion.1
  165.2 2.7 gather_fusion
  196.4 2.7 gather_fusion.1
  199.3 2.7 gather_fusion
  230.4 2.7 gather_fusion.1
  233.4 2.7 gather_fusion
  264.5 2.7 gather_fusion.1
  267.4 2.7 gather_fusion
  298.5 2.7 gather_fusion.1
  301.5 2.7 gather_fusion
  332.6 2.7 gather_fusion.1
  335.5 2.7 gather_fusion
  427.5 29.8 %all-reduce = (f32[3]{0:T(128)S(1)}, f32[3]{0:T(128)S(1)}) all-reduce(f32[3]{0:T(128)} %broadcast_multiply_fusion, f32[3]{0:T(128)} %get-tuple-element.496), channel_id=1, replica_groups=mesh['rep'=2,'gx'=16] {'gx'}, use_global_device_ids=true, to_apply=%region_13.15 | all-reduce | flops 6 | bytes 48 | tf_op jit(solution)/shard_map/psum | solution.py:77
  462.3 4.7 %collective-permute-done.2 = f32[24,192]{0,1:T(8,128)S(1)} collective-permute-done((f32[24,192]{0,1:T(8,128)S(1)}, f32[24,192]{0,1:T(8,128)S(1)}, u32[]{:S(2)}, u32[]{:S(2)}) %collective-permute-start.2) | collective-permute-done | bytes 18464 | tf_op jit(solution)/shard_map/ppermute | solution.py:18
  (785 shorter events, 368.6 us)
Async XLA Ops:
  1.4 14.6 %collective-permute-start = (f32[6,1536]{1,0:T(8,128)S(1)}, f32[6,1536]{1,0:T(8,128)S(1)}, u32[]{:S(2)}, u32[]{:S(2)}) collective-permute-start(f32[6,1536]{1,0:T(8,128)S(1)} %pad_maximum_fusion.1), channel_id=1, source_target_pairs={{0,15},{1,0},{2,1},{3,2},{4,3},{5,4},{6,5},{7,6},{8,7},{9,8},{10,9... | collective-permute-start | bytes 110600 | tf_op jit(solution)/shard_map/ppermute | solution.py:18
  8.5 7.7 %copy-start.4 = (f32[3,1536]{1,0:T(4,128)S(1)}, f32[3,1536]{1,0:T(4,128)}, u32[]{:S(2)}) copy-start(f32[3,1536]{1,0:T(4,128)} %param.17) | copy-start | bytes 55300
  9.8 6.0 %collective-permute-start.1 = (f32[6,768]{1,0:T(8,128)S(1)}, f32[6,768]{1,0:T(8,128)S(1)}, u32[]{:S(2)}, u32[]{:S(2)}) collective-permute-start(f32[6,768]{1,0:T(8,128)S(1)} %reshape.315), channel_id=1, source_target_pairs={{0,14},{1,15},{2,0},{3,1},{4,2},{5,3},{6,4},{7,5},{8,6},{9,7},{10,... | collective-permute-start | bytes 55304 | tf_op jit(solution)/shard_map/ppermute | solution.py:18
  10.5 5.5 %copy-start.15 = (f32[1536]{0:T(1024)}, f32[1536]{0:T(1024)S(1)}, u32[]{:S(2)}) copy-start(f32[1536]{0:T(1024)S(1)} %slice_reduce_fusion) | copy-start | bytes 18436
  45.7 4.0 copy-start.7
  46.4 6.4 %copy-start.14 = (f32[3]{0:T(128)S(1)}, f32[3]{0:T(128)}, u32[]{:S(2)}) copy-start(f32[3]{0:T(128)} %get-tuple-element.509) | copy-start | bytes 40 | tf_op jit(solution)/shard_map/while
  80.5 6.4 %copy-start.14 = (f32[3]{0:T(128)S(1)}, f32[3]{0:T(128)}, u32[]{:S(2)}) copy-start(f32[3]{0:T(128)} %get-tuple-element.509) | copy-start | bytes 40 | tf_op jit(solution)/shard_map/while
  114.6 6.4 %copy-start.14 = (f32[3]{0:T(128)S(1)}, f32[3]{0:T(128)}, u32[]{:S(2)}) copy-start(f32[3]{0:T(128)} %get-tuple-element.509) | copy-start | bytes 40 | tf_op jit(solution)/shard_map/while
  148.7 6.4 %copy-start.14 = (f32[3]{0:T(128)S(1)}, f32[3]{0:T(128)}, u32[]{:S(2)}) copy-start(f32[3]{0:T(128)} %get-tuple-element.509) | copy-start | bytes 40 | tf_op jit(solution)/shard_map/while
  182.7 6.4 %copy-start.14 = (f32[3]{0:T(128)S(1)}, f32[3]{0:T(128)}, u32[]{:S(2)}) copy-start(f32[3]{0:T(128)} %get-tuple-element.509) | copy-start | bytes 40 | tf_op jit(solution)/shard_map/while
  216.1 4.0 copy-start.7
  216.8 6.4 %copy-start.14 = (f32[3]{0:T(128)S(1)}, f32[3]{0:T(128)}, u32[]{:S(2)}) copy-start(f32[3]{0:T(128)} %get-tuple-element.509) | copy-start | bytes 40 | tf_op jit(solution)/shard_map/while
  250.8 6.4 %copy-start.14 = (f32[3]{0:T(128)S(1)}, f32[3]{0:T(128)}, u32[]{:S(2)}) copy-start(f32[3]{0:T(128)} %get-tuple-element.509) | copy-start | bytes 40 | tf_op jit(solution)/shard_map/while
  284.9 6.4 %copy-start.14 = (f32[3]{0:T(128)S(1)}, f32[3]{0:T(128)}, u32[]{:S(2)}) copy-start(f32[3]{0:T(128)} %get-tuple-element.509) | copy-start | bytes 40 | tf_op jit(solution)/shard_map/while
  318.2 4.0 copy-start.7
  318.9 6.4 %copy-start.14 = (f32[3]{0:T(128)S(1)}, f32[3]{0:T(128)}, u32[]{:S(2)}) copy-start(f32[3]{0:T(128)} %get-tuple-element.509) | copy-start | bytes 40 | tf_op jit(solution)/shard_map/while
  353.0 6.4 %copy-start.14 = (f32[3]{0:T(128)S(1)}, f32[3]{0:T(128)}, u32[]{:S(2)}) copy-start(f32[3]{0:T(128)} %get-tuple-element.509) | copy-start | bytes 40 | tf_op jit(solution)/shard_map/while
  387.1 6.4 %copy-start.14 = (f32[3]{0:T(128)S(1)}, f32[3]{0:T(128)}, u32[]{:S(2)}) copy-start(f32[3]{0:T(128)} %get-tuple-element.509) | copy-start | bytes 40 | tf_op jit(solution)/shard_map/while
  421.1 6.4 %copy-start.14 = (f32[3]{0:T(128)S(1)}, f32[3]{0:T(128)}, u32[]{:S(2)}) copy-start(f32[3]{0:T(128)} %get-tuple-element.509) | copy-start | bytes 40 | tf_op jit(solution)/shard_map/while
  427.5 43.2 %copy-start.5 = (f32[3,1536]{1,0:T(4,128)S(1)}, f32[3,1536]{1,0:T(4,128)}, u32[]{:S(2)}) copy-start(f32[3,1536]{1,0:T(4,128)} %param.17) | copy-start | bytes 55300
  427.5 43.2 %copy-start.12 = (f32[3,1536]{1,0:T(4,128)S(1)}, f32[3,1536]{1,0:T(4,128)}, u32[]{:S(2)}) copy-start(f32[3,1536]{1,0:T(4,128)} %param.18) | copy-start | bytes 55300
  427.5 43.2 %copy-start.16 = (f32[1536]{0:T(1024)S(1)}, f32[1536]{0:T(1024)}, u32[]{:S(2)}) copy-start(f32[1536]{0:T(1024)} %copy-done.15) | copy-start | bytes 18436
  460.2 6.8 %collective-permute-start.2 = (f32[24,192]{0,1:T(8,128)S(1)}, f32[24,192]{0,1:T(8,128)S(1)}, u32[]{:S(2)}, u32[]{:S(2)}) collective-permute-start(f32[24,192]{0,1:T(8,128)S(1)} %slice.250), channel_id=1, source_target_pairs={{0,1},{1,2},{2,3},{3,4},{4,5},{5,6},{6,7},{7,8},{8,9},{9,10},{10,1... | collective-permute-start | bytes 55304 | tf_op jit(solution)/shard_map/ppermute | solution.py:18
  462.3 6.8 %collective-permute-start.3 = (f32[24,96]{0,1:T(8,128)S(1)}, f32[24,96]{0,1:T(8,128)S(1)}, u32[]{:S(2)}, u32[]{:S(2)}) collective-permute-start(f32[24,96]{0,1:T(8,128)S(1)} %slice.251), channel_id=1, source_target_pairs={{0,2},{1,3},{2,4},{3,5},{4,6},{5,7},{6,8},{7,9},{8,10},{9,11},{10,... | collective-permute-start | bytes 27656 | tf_op jit(solution)/shard_map/ppermute | solution.py:18
  (110 other events, 220.8 us)
where the time goes:
time: 478 us; the launch traced here: 471 us
  local copies, waits for them, and re-layouts  263 us (55%)
  other arithmetic  127 us (27%)
  matrix products  30.1 us (6%)
  blocking collectives  29.8 us (6%)
  between operations  6.79 us (1%)
  waiting for transfers between devices  6.77 us (1%)
  starting transfers between devices  6.18 us (1%)
    slice x48, local copies, waits for them, and re-layouts, pair_tiles(): charge_pair = first_rows[3][:, None, :] * second_rows[3][None, :, :]  61.5 us
    slice x24, local copies, waits for them, and re-layouts, pair_tiles(): dispersion = first_rows[4][:, None, :] * second_rows[4][None, :, :]  40.2 us
    gather x12, local copies, waits for them, and re-layouts, pair_tiles(): jnp.take(slot_table, pair_rows[0], axis=0).T.reshape(6, 8, tile_width)  32.3 us
    gather x12, local copies, waits for them, and re-layouts, pair_tiles(): jnp.take(slot_table, pair_rows[1], axis=0).T.reshape(6, 8, tile_width)  32.3 us
    slice x24, local copies, waits for them, and re-layouts, pair_tiles(): delta_z = second_rows[2][None, :, :] - first_rows[2][:, None, :] + image_z  32 us
    dot_general x12, matrix products, one_block(): jnp.dot(selector, tile_terms, precision=lax.Precision.HIGHEST, preferred_...  30.1 us
    psum x1, blocking collectives, on_device(): overall_motion_work = lax.psum(kinetic, 'gx')  29.8 us
    add x12, other arithmetic, one_block(): return (accumulated, virial + partial_value)  25 us
  transfers between devices with their start and end apart: 4, of which 2 were waited for; matrix products, arithmetic and copies ran while one was open for 1% of the time, Pallas kernels for 0%

commit v1 on v0

--- a/solution.py
+++ b/solution.py
@@ -74,7 +74,7 @@
     axis_count = lax.axis_size("gx")
     inverse_mass = atom_params[3]
     kinetic = 0.5 * jnp.sum(velocities * velocities / inverse_mass[None, :], axis=1)
-    overall_motion_work = lax.psum(kinetic, "gx")
+    overall_motion_work = jnp.sum(lax.all_gather(kinetic, "gx"), axis=0)
     packed = jnp.concatenate([positions, atom_params[:3]], axis=0)
     far_rows = packed.reshape(6, clusters, 8)[:, halo_far, :].reshape(6, far_clusters * 8)
     near_rows = passed_along(packed, "gx", -1)

time: 478 us -> 479 us (level)
    psum x1 -> x0, blocking collectives: 29.8 us -> none  [on_device(): overall_motion_work = lax.psum(kinetic, 'gx')]
    unnamed x0 -> x1, blocking collectives: none -> 29.8 us
where the time goes in v1:
time: 479 us; the launch traced here: 472 us
  local copies, waits for them, and re-layouts  263 us (55%)
  other arithmetic  126 us (26%)
  matrix products  30.1 us (6%)
  blocking collectives  29.8 us (6%)
  between operations  7.49 us (2%)
  waiting for transfers between devices  6.77 us (1%)
  starting transfers between devices  6.18 us (1%)
    slice x48, local copies, waits for them, and re-layouts, pair_tiles(): charge_pair = first_rows[3][:, None, :] * second_rows[3][None, :, :]  61.5 us
    slice x24, local copies, waits for them, and re-layouts, pair_tiles(): dispersion = first_rows[4][:, None, :] * second_rows[4][None, :, :]  40.2 us
    gather x12, local copies, waits for them, and re-layouts, pair_tiles(): jnp.take(slot_table, pair_rows[0], axis=0).T.reshape(6, 8, tile_width)  32.3 us
    gather x12, local copies, waits for them, and re-layouts, pair_tiles(): jnp.take(slot_table, pair_rows[1], axis=0).T.reshape(6, 8, tile_width)  32.3 us
    slice x24, local copies, waits for them, and re-layouts, pair_tiles(): delta_z = second_rows[2][None, :, :] - first_rows[2][:, None, :] + image_z  32 us
    dot_general x12, matrix products, one_block(): jnp.dot(selector, tile_terms, precision=lax.Precision.HIGHEST, preferred_...  30.1 us
    unnamed x1, blocking collectives  29.8 us
    add x12, other arithmetic, one_block(): return (accumulated, virial + partial_value)  25 us
  transfers between devices with their start and end apart: 4, of which 2 were waited for; matrix products, arithmetic and copies ran while one was open for 1% of the time, Pallas kernels for 0%

profile of v1, /device:TPU:0, one launch (start us, length us, event | category | flops | bytes accessed | tf_op | source)
XLA Modules:
  0.0 472.4 jit_solution(16696163150835289652)
XLA Ops:
  1.4 5.5 %collective-permute-start = (f32[6,1536]{1,0:T(8,128)S(1)}, f32[6,1536]{1,0:T(8,128)S(1)}, u32[]{:S(2)}, u32[]{:S(2)}) collective-permute-start(f32[6,1536]{1,0:T(8,128)S(1)} %pad_maximum_fusion.1), channel_id=1, source_target_pairs={{0,15},{1,0},{2,1},{3,2},{4,3},{5,4},{6,5},{7,6},{8,7},{9,8},{10,9... | collective-permute-start | bytes 110600 | tf_op jit(solution)/shard_map/ppermute | solution.py:18
  19.6 408.8 %while.18 = (s32[]{:T(128)}, f32[480,24]{0,1:T(8,128)}, f32[3]{0:T(128)}, s32[]{:T(128)}, s32[3,16896]{1,0:T(4,128)}, /*index=5*/s32[4,16896]{1,0:T(4,128)}, s32...) while((s32[]{:T(128)}, f32[480,24]{0,1:T(8,128)}, ...), condition=%wide.region_10.12_spmd.clone, body=%wide.region_0.11_spmd.clone.sunk | while | flops 397501280 | bytes 8990699 | solution.py:109
  26.8 2.7 gather_fusion.1
  29.8 2.7 gather_fusion
  60.9 2.7 gather_fusion.1
  63.8 2.7 gather_fusion
  95.0 2.7 gather_fusion.1
  97.9 2.7 gather_fusion
  129.0 2.7 gather_fusion.1
  132.0 2.7 gather_fusion
  163.1 2.7 gather_fusion.1
  166.1 2.7 gather_fusion
  197.2 2.7 gather_fusion.1
  200.1 2.7 gather_fusion
  231.2 2.7 gather_fusion.1
  234.2 2.7 gather_fusion
  265.3 2.7 gather_fusion.1
  268.2 2.7 gather_fusion
  299.3 2.7 gather_fusion.1
  302.3 2.7 gather_fusion
  333.4 2.7 gather_fusion.1
  370.4 2.7 gather_fusion
  428.3 29.8 %all-reduce.1 = (f32[48]{0:T(128)S(1)}, f32[3]{0:T(128)S(1)}) all-reduce(f32[48]{0:T(128)} %copy-done.21, f32[3]{0:T(128)} %get-tuple-element.496), channel_id=2, replica_groups=mesh['rep'=2,'gx'=16] {'gx'}, use_global_device_ids=true, to_apply=%add | all-reduce | flops 51 | bytes 408
  463.2 4.7 %collective-permute-done.2 = f32[24,192]{0,1:T(8,128)S(1)} collective-permute-done((f32[24,192]{0,1:T(8,128)S(1)}, f32[24,192]{0,1:T(8,128)S(1)}, u32[]{:S(2)}, u32[]{:S(2)}) %collective-permute-start.2) | collective-permute-done | bytes 18464 | tf_op jit(solution)/shard_map/ppermute | solution.py:18
  (793 shorter events, 368.8 us)
Async XLA Ops:
  1.4 15.4 %collective-permute-start = (f32[6,1536]{1,0:T(8,128)S(1)}, f32[6,1536]{1,0:T(8,128)S(1)}, u32[]{:S(2)}, u32[]{:S(2)}) collective-permute-start(f32[6,1536]{1,0:T(8,128)S(1)} %pad_maximum_fusion.1), channel_id=1, source_target_pairs={{0,15},{1,0},{2,1},{3,2},{4,3},{5,4},{6,5},{7,6},{8,7},{9,8},{10,9... | collective-permute-start | bytes 110600 | tf_op jit(solution)/shard_map/ppermute | solution.py:18
  8.5 8.4 %copy-start.4 = (f32[3,1536]{1,0:T(4,128)S(1)}, f32[3,1536]{1,0:T(4,128)}, u32[]{:S(2)}) copy-start(f32[3,1536]{1,0:T(4,128)} %param.17) | copy-start | bytes 55300
  9.8 6.8 %collective-permute-start.1 = (f32[6,768]{1,0:T(8,128)S(1)}, f32[6,768]{1,0:T(8,128)S(1)}, u32[]{:S(2)}, u32[]{:S(2)}) collective-permute-start(f32[6,768]{1,0:T(8,128)S(1)} %reshape.324), channel_id=1, source_target_pairs={{0,14},{1,15},{2,0},{3,1},{4,2},{5,3},{6,4},{7,5},{8,6},{9,7},{10,... | collective-permute-start | bytes 55304 | tf_op jit(solution)/shard_map/ppermute | solution.py:18
  10.5 6.3 %copy-start.15 = (f32[1536]{0:T(1024)}, f32[1536]{0:T(1024)S(1)}, u32[]{:S(2)}) copy-start(f32[1536]{0:T(1024)S(1)} %slice_reduce_fusion) | copy-start | bytes 18436
  12.0 4.6 copy-start.21
  46.5 4.0 copy-start.7
  47.2 6.4 %copy-start.14 = (f32[3]{0:T(128)S(1)}, f32[3]{0:T(128)}, u32[]{:S(2)}) copy-start(f32[3]{0:T(128)} %get-tuple-element.509) | copy-start | bytes 40 | tf_op jit(solution)/shard_map/while
  81.3 6.4 %copy-start.14 = (f32[3]{0:T(128)S(1)}, f32[3]{0:T(128)}, u32[]{:S(2)}) copy-start(f32[3]{0:T(128)} %get-tuple-element.509) | copy-start | bytes 40 | tf_op jit(solution)/shard_map/while
  115.4 6.4 %copy-start.14 = (f32[3]{0:T(128)S(1)}, f32[3]{0:T(128)}, u32[]{:S(2)}) copy-start(f32[3]{0:T(128)} %get-tuple-element.509) | copy-start | bytes 40 | tf_op jit(solution)/shard_map/while
  149.5 6.4 %copy-start.14 = (f32[3]{0:T(128)S(1)}, f32[3]{0:T(128)}, u32[]{:S(2)}) copy-start(f32[3]{0:T(128)} %get-tuple-element.509) | copy-start | bytes 40 | tf_op jit(solution)/shard_map/while
  183.5 6.4 %copy-start.14 = (f32[3]{0:T(128)S(1)}, f32[3]{0:T(128)}, u32[]{:S(2)}) copy-start(f32[3]{0:T(128)} %get-tuple-element.509) | copy-start | bytes 40 | tf_op jit(solution)/shard_map/while
  217.6 6.4 %copy-start.14 = (f32[3]{0:T(128)S(1)}, f32[3]{0:T(128)}, u32[]{:S(2)}) copy-start(f32[3]{0:T(128)} %get-tuple-element.509) | copy-start | bytes 40 | tf_op jit(solution)/shard_map/while
  251.7 6.4 %copy-start.14 = (f32[3]{0:T(128)S(1)}, f32[3]{0:T(128)}, u32[]{:S(2)}) copy-start(f32[3]{0:T(128)} %get-tuple-element.509) | copy-start | bytes 40 | tf_op jit(solution)/shard_map/while
  285.7 6.4 %copy-start.14 = (f32[3]{0:T(128)S(1)}, f32[3]{0:T(128)}, u32[]{:S(2)}) copy-start(f32[3]{0:T(128)} %get-tuple-element.509) | copy-start | bytes 40 | tf_op jit(solution)/shard_map/while
  319.8 6.4 %copy-start.14 = (f32[3]{0:T(128)S(1)}, f32[3]{0:T(128)}, u32[]{:S(2)}) copy-start(f32[3]{0:T(128)} %get-tuple-element.509) | copy-start | bytes 40 | tf_op jit(solution)/shard_map/while
  353.8 6.4 %copy-start.14 = (f32[3]{0:T(128)S(1)}, f32[3]{0:T(128)}, u32[]{:S(2)}) copy-start(f32[3]{0:T(128)} %get-tuple-element.509) | copy-start | bytes 40 | tf_op jit(solution)/shard_map/while
  387.2 4.0 copy-start.7
  387.9 6.4 %copy-start.14 = (f32[3]{0:T(128)S(1)}, f32[3]{0:T(128)}, u32[]{:S(2)}) copy-start(f32[3]{0:T(128)} %get-tuple-element.509) | copy-start | bytes 40 | tf_op jit(solution)/shard_map/while
  421.9 6.4 %copy-start.14 = (f32[3]{0:T(128)S(1)}, f32[3]{0:T(128)}, u32[]{:S(2)}) copy-start(f32[3]{0:T(128)} %get-tuple-element.509) | copy-start | bytes 40 | tf_op jit(solution)/shard_map/while
  428.3 43.3 %copy-start.5 = (f32[3,1536]{1,0:T(4,128)S(1)}, f32[3,1536]{1,0:T(4,128)}, u32[]{:S(2)}) copy-start(f32[3,1536]{1,0:T(4,128)} %param.17) | copy-start | bytes 55300
  428.3 43.3 %copy-start.12 = (f32[3,1536]{1,0:T(4,128)S(1)}, f32[3,1536]{1,0:T(4,128)}, u32[]{:S(2)}) copy-start(f32[3,1536]{1,0:T(4,128)} %param.18) | copy-start | bytes 55300
  428.3 43.3 %copy-start.16 = (f32[1536]{0:T(1024)S(1)}, f32[1536]{0:T(1024)}, u32[]{:S(2)}) copy-start(f32[1536]{0:T(1024)} %copy-done.15) | copy-start | bytes 18436
  461.1 6.8 %collective-permute-start.2 = (f32[24,192]{0,1:T(8,128)S(1)}, f32[24,192]{0,1:T(8,128)S(1)}, u32[]{:S(2)}, u32[]{:S(2)}) collective-permute-start(f32[24,192]{0,1:T(8,128)S(1)} %slice.250), channel_id=1, source_target_pairs={{0,1},{1,2},{2,3},{3,4},{4,5},{5,6},{6,7},{7,8},{8,9},{9,10},{10,1... | collective-permute-start | bytes 55304 | tf_op jit(solution)/shard_map/ppermute | solution.py:18
  463.2 6.8 %collective-permute-start.3 = (f32[24,96]{0,1:T(8,128)S(1)}, f32[24,96]{0,1:T(8,128)S(1)}, u32[]{:S(2)}, u32[]{:S(2)}) collective-permute-start(f32[24,96]{0,1:T(8,128)S(1)} %slice.251), channel_id=1, source_target_pairs={{0,2},{1,3},{2,4},{3,5},{4,6},{5,7},{6,8},{7,9},{8,10},{9,11},{10,... | collective-permute-start | bytes 27656 | tf_op jit(solution)/shard_map/ppermute | solution.py:18
  (112 other events, 228.9 us)
